TPU v7x, 32 devices: a whole 2x2x4 slice. The times are simulated.
32 devices in a mesh: row: 16 (over z, y, x), col: 2 (over core).
Axes of the slice: x: 2, y: 2, z: 4, core: 2. Of those that a mesh axis runs over, the one named last changes fastest.
Arguments:
- incident: bfloat16 [2, 8192, 512], P(None, ('row', 'col')), may hold values from -6 to 6
- near_tiles: bfloat16 [32, 2, 3, 2, 256, 256], P(('row', 'col')), may hold values from -0.15625 to 0.15625
- near_offsets: int32 [32, 3], P(('row', 'col')), may hold values from -2 to 2, as said below
- far_row: int32 [16, 2, 16], P('row', 'col'), may hold values from 0 to 1, as said below
- far_col: int32 [16, 2, 16], P('row', 'col'), may hold values from 0 to 15
- far_rank: int32 [16, 2, 16], P('row', 'col'), may hold values from 8 to 32, as said below
- far_count: int32 [16, 2], P('row', 'col'), may hold values from 2 to 16, as said below
- far_u: bfloat16 [16, 2, 2, 16, 2, 32, 256], P('row', 'col'), may hold values from -0.25 to 0.25
- far_v: bfloat16 [16, 2, 2, 16, 2, 32, 256], P('row', 'col'), may hold values from -0.25 to 0.25
Outputs:
- response: bfloat16 [2, 8192, 512], P(None, ('row', 'col'))
Inputs may be any that keep to these rules, and one draw needn't show every extreme that they name: `near_offsets`: slot 0 of every tile is 0; the other slots of a tile hold distinct values among -2, -1, 1, 2. On one device the pairs (far_row, far_col) of all 16 slots are distinct, and every block (i, j) they name has circular tile distance 3 or more between i and j. `far_rank`: slot 0 of every device has rank 32. `far_count`: some device has all 16 slots live.
All inputs are finite; a program needn't handle non-finite values.
Results may differ from a plain program's by a relative error of at most 0.0035.
Values may be sent and summed in bfloat16 or wider, within the bound.
A program may use at most 192 MiB of HBM per device.

v0:
```python
import jax
import jax.numpy as jnp
from jax import lax
from jax.sharding import PartitionSpec as P


def from_behind(value, axis, steps):
    count = lax.axis_size(axis)
    pairs = [(source, (source + steps) % count) for source in range(count)]
    return lax.ppermute(value, axis, pairs)


def combine_parts(real_prod, imag_prod):
    half_width = real_prod.shape[-1] // 2
    return jnp.concatenate(
        [
            real_prod[..., :half_width] - imag_prod[..., half_width:],
            real_prod[..., half_width:] + imag_prod[..., :half_width],
        ],
        axis=-1,
    )


def far_partial(
    wave_tiles,
    rows_local,
    cols_local,
    rank_local,
    live_count,
    u_wave,
    v_wave,
    group_limit,
    row_blocks,
):
    group_size = 16
    tile_rows = wave_tiles.shape[1]
    columns = wave_tiles.shape[2]
    rank_size = v_wave.shape[2]
    slot_ids = jnp.arange(group_size, dtype=jnp.int32)
    rank_ids = jnp.arange(rank_size, dtype=jnp.int32)

    def add_group(group_step, far_sum):
        first_slot = group_step * group_size
        rows_group = lax.dynamic_slice_in_dim(rows_local, first_slot, group_size)
        cols_group = lax.dynamic_slice_in_dim(cols_local, first_slot, group_size)
        rank_group = lax.dynamic_slice_in_dim(rank_local, first_slot, group_size)
        v_group = lax.dynamic_slice_in_dim(v_wave, first_slot, group_size, 0)
        u_group = lax.dynamic_slice_in_dim(u_wave, first_slot, group_size, 0)
        slot_tiles = jnp.take(wave_tiles, cols_group, axis=0)
        real_prod = jnp.einsum(
            "fkq,fqc->fkc", v_group[:, 0], slot_tiles, preferred_element_type=jnp.float32
        )
        imag_prod = jnp.einsum(
            "fkq,fqc->fkc", v_group[:, 1], slot_tiles, preferred_element_type=jnp.float32
        )
        live_mask = (first_slot + slot_ids < live_count)[:, None] & (
            rank_ids[None, :] < rank_group[:, None]
        )
        coefficients = (
            combine_parts(real_prod, imag_prod) * live_mask[:, :, None].astype(jnp.float32)
        ).astype(jnp.bfloat16)
        real_back = jnp.einsum(
            "fkp,fkc->fpc", u_group[:, 0], coefficients, preferred_element_type=jnp.float32
        )
        imag_back = jnp.einsum(
            "fkp,fkc->fpc", u_group[:, 1], coefficients, preferred_element_type=jnp.float32
        )
        contrib = combine_parts(real_back, imag_back)
        return far_sum.at[rows_group].add(contrib)

    zero_sum = jnp.zeros((row_blocks, tile_rows, columns), jnp.float32)
    return lax.fori_loop(0, group_limit, add_group, zero_sum)


def reduce_rows(far_sum, row_blocks, tile_rows, columns):
    flat_rows = far_sum.reshape(row_blocks * tile_rows, columns)
    return lax.psum_scatter(flat_rows, "col", scatter_dimension=0, tiled=True)


def shards(incident, near_tiles, near_offsets, far_row, far_col, far_rank, far_count, far_u, far_v):
    wave_count, tile_rows, columns = incident.shape
    row_blocks = lax.axis_size("col")
    slot_count = far_row.shape[2]
    stacked = []
    for shift_by in (2, 1, 0, -1, -2):
        if shift_by == 0:
            stacked.append(incident)
        else:
            stacked.append(from_behind(incident, ("row", "col"), shift_by))
    neighbour = jnp.stack(stacked, axis=1)
    near_inputs = jnp.take(neighbour, near_offsets[0] + 2, axis=1)
    local_near = near_tiles[0]
    real_prod = jnp.einsum(
        "wnpq,wnqc->wpc", local_near[:, :, 0], near_inputs, preferred_element_type=jnp.float32
    )
    imag_prod = jnp.einsum(
        "wnpq,wnqc->wpc", local_near[:, :, 1], near_inputs, preferred_element_type=jnp.float32
    )
    near_total = combine_parts(real_prod, imag_prod)
    rows_local = far_row[0, 0]
    cols_local = far_col[0, 0]
    rank_local = far_rank[0, 0]
    live_count = far_count[0, 0]
    group_limit = slot_count // 16
    gathered = lax.all_gather(incident, "row", axis=1, tiled=True)
    outputs = []
    for wave_index in range(wave_count):
        wave_columns = gathered[wave_index]
        wave_tiles = wave_columns.reshape(-1, tile_rows, columns)
        far_sum = far_partial(
            wave_tiles,
            rows_local,
            cols_local,
            rank_local,
            live_count,
            far_u[0, 0, wave_index],
            far_v[0, 0, wave_index],
            group_limit,
            row_blocks,
        )
        own_rows = reduce_rows(far_sum, row_blocks, tile_rows, columns)
        outputs.append(near_total[wave_index] + own_rows)
    return jnp.stack(outputs, axis=0).astype(jnp.bfloat16)


def solution(mesh):
    in_specs = (
        P(None, ("row", "col"), None),
        P(("row", "col"), None, None, None, None, None),
        P(("row", "col"), None),
        P("row", "col", None),
        P("row", "col", None),
        P("row", "col", None),
        P("row", "col"),
        P("row", "col", None, None, None, None, None),
        P("row", "col", None, None, None, None, None),
    )
    out_specs = P(None, ("row", "col"), None)
    return jax.shard_map(shards, mesh=mesh, in_specs=in_specs, out_specs=out_specs, check_vma=False)
```

profile of v0, /device:TPU:0, one launch (start us, length us, event | category | flops | bytes accessed | tf_op | source)
XLA Modules:
  0.0 278.1 jit_solution(9200736228091735407)
XLA Ops:
  7.3 6.5 %collective-permute-start.2 = (bf16[2,256,512]{2,1,0:T(8,128)(2,1)}, bf16[2,256,512]{2,1,0:T(8,128)(2,1)}, u32[]{:S(2)}, u32[]{:S(2)}) collective-permute-start(bf16[2,256,512]{2,1,0:T(8,128)(2,1)} %param.11), channel_id=1, source_target_pairs={{0,31},{1,0},{2,1},{3,2},{4,3},{5,4},{6,5},{7,6},{8,7},{9,8},{10,9... | collective-permute-start | bytes 1572872 | tf_op jit(solution)/shard_map/ppermute | solution.py:10
  13.8 5.6 %collective-permute-start.3 = (bf16[2,256,512]{2,1,0:T(8,128)(2,1)}, bf16[2,256,512]{2,1,0:T(8,128)(2,1)}, u32[]{:S(2)}, u32[]{:S(2)}) collective-permute-start(bf16[2,256,512]{2,1,0:T(8,128)(2,1)} %param.11), channel_id=1, source_target_pairs={{0,30},{1,31},{2,0},{3,1},{4,2},{5,3},{6,4},{7,5},{8,6},{9,7},{10,... | collective-permute-start | bytes 1572872 | tf_op jit(solution)/shard_map/ppermute | solution.py:10
  20.0 1.6 copy.49
  26.1 1.1 copy_bitcast_fusion.2
  28.1 107.7 %all-gather.2.cloned.1.call-done = bf16[2,4096,512]{2,1,0:T(8,128)(2,1)} async-done(((bf16[2,256,512]{2,1,0:T(8,128)(2,1)}), bf16[2,4096,512]{2,1,0:T(8,128)(2,1)}) %all-gather.2.cloned.1.call-update) | async-done | bytes 8388624 | tf_op jit(solution)/shard_map/all_gather | solution.py:105
  135.9 5.7 %fusion.49 = (bf16[1,4096,512]{2,1,0:T(8,128)(2,1)}, bf16[1,4096,512]{2,1,0:T(8,128)(2,1)}) fusion(bf16[2,4096,512]{2,1,0:T(8,128)(2,1)} %all-gather.2.cloned.1.call-done), kind=kLoop, calls=%fused_computation.101 | loop fusion | bytes 16777216 | tf_op jit(solution)/shard_map/slice | solution.py:108
  141.6 5.0 %gather_fusion.2 = bf16[16,256,512]{2,1,0:T(8,128)(2,1)} fusion(bf16[16,256,512]{2,1,0:T(8,128)(2,1)} %bitcast.130, s32[1024]{0:T(1024)S(1)} %pad_clamp_fusion), kind=kCustom, calls=%fused_computation.1.clone | custom fusion | bytes 8388672 | tf_op jit(solution)/shard_map/while/body/eval_jaxpr/jit(_take)/gather | solution.py:49
  146.6 3.4 %fusion.14 = f32[16,32,512]{2,1,0:T(8,128)S(1)} fusion(bf16[16,256,512]{2,1,0:T(8,128)(2,1)} %gather_fusion.2, pred[16]{0:T(512)(128)(4,1)S(1)} %compare_and_fusion, bf16[16,2,32,256]{3,2,0,1:T(8,128)(2,1)S(1)} %copy-done.7), kind=kOutput, calls=%fused_computation.29 | convolution fusion | flops 136314880 | bytes 5505536 | tf_op jit(solution)/shard_map/while/body/eval_jaxpr/fkq,fqc->fkc/dot_general | solution.py:53
  150.1 2.0 fusion.15
  152.1 5.0 %gather_fusion.1 = bf16[16,256,512]{2,1,0:T(8,128)(2,1)} fusion(bf16[16,256,512]{2,1,0:T(8,128)(2,1)} %bitcast.129, s32[1024]{0:T(1024)S(1)} %pad_clamp_fusion), kind=kCustom, calls=%fused_computation.clone | custom fusion | bytes 8388672 | tf_op jit(solution)/shard_map/while/body/eval_jaxpr/jit(_take)/gather | solution.py:49
  157.1 3.4 %fusion.16 = f32[16,32,512]{2,1,0:T(8,128)S(1)} fusion(bf16[16,256,512]{2,1,0:T(8,128)(2,1)} %gather_fusion.1, pred[16]{0:T(512)(128)(4,1)S(1)} %compare_and_fusion, bf16[16,2,32,256]{3,2,0,1:T(8,128)(2,1)S(1)} %copy-done.6), kind=kOutput, calls=%fused_computation.31 | convolution fusion | flops 136314880 | bytes 5505536 | tf_op jit(solution)/shard_map/while/body/eval_jaxpr/fkq,fqc->fkc/dot_general | solution.py:53
  161.8 4.8 %convolution_bitcast_fusion.2 = f32[16,256,512]{1,2,0:T(8,128)} fusion(bf16[16,2,32,256]{3,2,0,1:T(8,128)(2,1)S(1)} %get-tuple-element.98, f32[16,32,256]{2,1,0:T(8,128)S(1)} %get-tuple-element.59, f32[16,32,256]{2,1,0:T(8,128)S(1)} %get-tuple-element.58, f32[16,32]{1,0:T(8,128)S(1)} %fusion.36), kind=kOutput, calls=%fused_computation.15 | convolution fusion | flops 135004160 | bytes 9707520 | tf_op jit(solution)/shard_map/while/body/eval_jaxpr/fkp,fkc->fpc/dot_general | solution.py:65
  166.6 4.8 %convolution_bitcast_fusion.3 = f32[16,256,512]{1,2,0:T(8,128)} fusion(bf16[16,2,32,256]{3,2,0,1:T(8,128)(2,1)S(1)} %get-tuple-element.98, f32[16,32,256]{2,1,0:T(8,128)S(1)} %get-tuple-element.59, f32[16,32,256]{2,1,0:T(8,128)S(1)} %get-tuple-element.58, f32[16,32]{1,0:T(8,128)S(1)} %fusion.36), kind=kOutput, calls=%fused_computation.16 | convolution fusion | flops 135004160 | bytes 9707520 | tf_op jit(solution)/shard_map/while/body/eval_jaxpr/fkp,fkc->fpc/dot_general | solution.py:62
  171.5 9.2 %slice_subtract_fusion.1 = (f32[16,256,256]{1,2,0:T(8,128)S(1)}, f32[16,256,256]{1,2,0:T(8,128)}) fusion(f32[16,256,512]{1,2,0:T(8,128)} %convolution_bitcast_fusion.2, f32[16,256,512]{1,2,0:T(8,128)} %convolution_bitcast_fusion.3), kind=kLoop, calls=%fused_computation.10 | loop fusion | flops 2097152 | bytes 25165824 | tf_op jit(solution)/shard_map/while/body/eval_jaxpr/sub | solution.py:17
  180.6 6.2 %pad_maximum_fusion = f32[16,256,512]{1,2,0:T(8,128)} fusion(f32[16,256,256]{1,2,0:T(8,128)} %get-tuple-element.53, f32[16,256,256]{1,2,0:T(8,128)S(1)} %get-tuple-element.52), kind=kLoop, calls=%fused_computation.5 | loop fusion | flops 2097152 | bytes 16777216 | tf_op jit(solution)/shard_map/while/body/eval_jaxpr/concatenate | solution.py:15
  186.8 9.2 %copy.23 = f32[16,256,512]{2,1,0:T(8,128)} copy(f32[16,256,512]{1,2,0:T(8,128)} %pad_maximum_fusion) | data formatting | bytes 16777216 | tf_op jit(solution)/shard_map/while/body/eval_jaxpr/concatenate | solution.py:15
  196.2 10.8 %scatter_fusion = f32[2,256,512]{2,1,0:T(8,128)S(1)} fusion(f32[2,256,512]{2,1,0:T(8,128)S(1)} %broadcast.124.clone, s32[16]{0:T(128)S(1)} %fusion.38, f32[16,256,512]{2,1,0:T(8,128)} %copy.23), kind=kCustom, calls=%fused_computation.3 | custom fusion | flops 2097152 | bytes 25165888 | tf_op jit(solution)/shard_map/while/body/eval_jaxpr/scatter-add | solution.py:69
  207.0 1.3 copy.34
  208.5 1.3 slice_subtract_fusion.2
  209.9 4.9 %convolution_bitcast_fusion = f32[16,256,512]{1,2,0:T(8,128)} fusion(bf16[16,2,32,256]{3,2,0,1:T(8,128)(2,1)S(1)} %get-tuple-element.96, f32[16,32,256]{2,1,0:T(8,128)S(1)} %get-tuple-element.75, f32[16,32,256]{2,1,0:T(8,128)S(1)} %get-tuple-element.74, f32[16,32]{1,0:T(8,128)S(1)} %fusion.36), kind=kOutput, calls=%fused_computation.13 | convolution fusion | flops 135004160 | bytes 9707520 | tf_op jit(solution)/shard_map/while/body/eval_jaxpr/fkp,fkc->fpc/dot_general | solution.py:65
  214.8 4.8 %convolution_bitcast_fusion.1 = f32[16,256,512]{1,2,0:T(8,128)} fusion(bf16[16,2,32,256]{3,2,0,1:T(8,128)(2,1)S(1)} %get-tuple-element.96, f32[16,32,256]{2,1,0:T(8,128)S(1)} %get-tuple-element.75, f32[16,32,256]{2,1,0:T(8,128)S(1)} %get-tuple-element.74, f32[16,32]{1,0:T(8,128)S(1)} %fusion.36), kind=kOutput, calls=%fused_computation.14 | convolution fusion | flops 135004160 | bytes 9707520 | tf_op jit(solution)/shard_map/while/body/eval_jaxpr/fkp,fkc->fpc/dot_general | solution.py:62
  219.6 9.2 %slice_subtract_fusion = (f32[16,256,256]{1,2,0:T(8,128)S(1)}, f32[16,256,256]{1,2,0:T(8,128)}) fusion(f32[16,256,512]{1,2,0:T(8,128)} %convolution_bitcast_fusion, f32[16,256,512]{1,2,0:T(8,128)} %convolution_bitcast_fusion.1), kind=kLoop, calls=%fused_computation.8 | loop fusion | flops 2097152 | bytes 25165824 | tf_op jit(solution)/shard_map/while/body/eval_jaxpr/sub | solution.py:17
  228.8 6.2 %pad_maximum_fusion.1 = f32[16,256,512]{1,2,0:T(8,128)} fusion(f32[16,256,256]{1,2,0:T(8,128)} %get-tuple-element.55, f32[16,256,256]{1,2,0:T(8,128)S(1)} %get-tuple-element.54), kind=kLoop, calls=%fused_computation.6 | loop fusion | flops 2097152 | bytes 16777216 | tf_op jit(solution)/shard_map/while/body/eval_jaxpr/concatenate | solution.py:15
  235.0 9.2 %copy.27 = f32[16,256,512]{2,1,0:T(8,128)} copy(f32[16,256,512]{1,2,0:T(8,128)} %pad_maximum_fusion.1) | data formatting | bytes 16777216 | tf_op jit(solution)/shard_map/while/body/eval_jaxpr/concatenate | solution.py:15
  244.4 10.8 %scatter_fusion.1 = f32[2,256,512]{2,1,0:T(8,128)S(1)} fusion(f32[2,256,512]{2,1,0:T(8,128)S(1)} %broadcast.124.clone.1, s32[16]{0:T(128)S(1)} %fusion.38, f32[16,256,512]{2,1,0:T(8,128)} %copy.27), kind=kCustom, calls=%fused_computation.4 | custom fusion | flops 2097152 | bytes 25165888 | tf_op jit(solution)/shard_map/while/body/eval_jaxpr/scatter-add | solution.py:69
  255.2 1.3 copy.35
  256.5 2.0 bitcast_dynamic-update-slice_fusion.4
  258.5 1.9 bitcast_dynamic-update-slice_fusion.3
  261.2 1.9 bitcast_dynamic-update-slice_fusion.1
  263.1 1.9 bitcast_dynamic-update-slice_fusion
  264.9 2.4 gather_fusion
  269.2 1.3 fusion.30
  (53 shorter events, 11.7 us)
Async XLA Ops:
  6.5 19.2 %copy-start.3 = (bf16[1,1,2,16,2,32,256]{6,5,4,3,2,1,0:T(8,128)(2,1)S(1)}, bf16[1,1,2,16,2,32,256]{6,5,4,3,2,1,0:T(8,128)(2,1)}, u32[]{:S(2)}) copy-start(bf16[1,1,2,16,2,32,256]{6,5,4,3,2,1,0:T(8,128)(2,1)} %param.18) | copy-start | bytes 3145732
  6.5 19.3 %copy-start.4 = (bf16[1,1,2,16,2,32,256]{6,5,4,3,2,1,0:T(8,128)(2,1)S(1)}, bf16[1,1,2,16,2,32,256]{6,5,4,3,2,1,0:T(8,128)(2,1)}, u32[]{:S(2)}) copy-start(bf16[1,1,2,16,2,32,256]{6,5,4,3,2,1,0:T(8,128)(2,1)} %param.19) | copy-start | bytes 3145732
  6.5 129.3 %all-gather.2.cloned.1.call-start = ((), (), s32[]{:S(2)}) async-start(), calls=%async_computation.2 | async-start | bytes 8912896 | tf_op jit(solution)/shard_map/all_gather | solution.py:105
  7.3 261.9 %reduce-scatter.3.cloned.1.call-start = ((), (), s32[]{:S(2)}) async-start(), calls=%async_computation.3 | async-start | bytes 1572864 | tf_op jit(solution)/shard_map/reduce_scatter | solution.py:77
  7.3 253.9 %collective-permute-start.2 = (bf16[2,256,512]{2,1,0:T(8,128)(2,1)}, bf16[2,256,512]{2,1,0:T(8,128)(2,1)}, u32[]{:S(2)}, u32[]{:S(2)}) collective-permute-start(bf16[2,256,512]{2,1,0:T(8,128)(2,1)} %param.11), channel_id=1, source_target_pairs={{0,31},{1,0},{2,1},{3,2},{4,3},{5,4},{6,5},{7,6},{8,7},{9,8},{10,9... | collective-permute-start | bytes 1572872 | tf_op jit(solution)/shard_map/ppermute | solution.py:10
  13.8 244.7 %collective-permute-start.1 = (bf16[2,256,512]{2,1,0:T(8,128)(2,1)}, bf16[2,256,512]{2,1,0:T(8,128)(2,1)}, u32[]{:S(2)}, u32[]{:S(2)}) collective-permute-start(bf16[2,256,512]{2,1,0:T(8,128)(2,1)} %param.11), channel_id=1, source_target_pairs={{0,1},{1,2},{2,3},{3,4},{4,5},{5,6},{6,7},{7,8},{8,9},{9,10},{10,1... | collective-permute-start | bytes 1572872 | tf_op jit(solution)/shard_map/ppermute | solution.py:10
  13.8 242.7 %collective-permute-start = (bf16[2,256,512]{2,1,0:T(8,128)(2,1)}, bf16[2,256,512]{2,1,0:T(8,128)(2,1)}, u32[]{:S(2)}, u32[]{:S(2)}) collective-permute-start(bf16[2,256,512]{2,1,0:T(8,128)(2,1)} %param.11), channel_id=1, source_target_pairs={{0,2},{1,3},{2,4},{3,5},{4,6},{5,7},{6,8},{7,9},{8,10},{9,11},{10,... | collective-permute-start | bytes 1572872 | tf_op jit(solution)/shard_map/ppermute | solution.py:10
  13.8 249.3 %collective-permute-start.3 = (bf16[2,256,512]{2,1,0:T(8,128)(2,1)}, bf16[2,256,512]{2,1,0:T(8,128)(2,1)}, u32[]{:S(2)}, u32[]{:S(2)}) collective-permute-start(bf16[2,256,512]{2,1,0:T(8,128)(2,1)} %param.11), channel_id=1, source_target_pairs={{0,30},{1,31},{2,0},{3,1},{4,2},{5,3},{6,4},{7,5},{8,6},{9,7},{10,... | collective-permute-start | bytes 1572872 | tf_op jit(solution)/shard_map/ppermute | solution.py:10
  141.6 5.0 %copy-start.7 = (bf16[16,2,32,256]{3,2,0,1:T(8,128)(2,1)S(1)}, bf16[16,2,32,256]{3,2,0,1:T(8,128)(2,1)}, u32[]{:S(2)}) copy-start(bf16[16,2,32,256]{3,2,0,1:T(8,128)(2,1)} %get-tuple-element.100) | copy-start | bytes 1572868
  146.6 3.4 %copy-start.1 = (bf16[16,256,512]{2,1,0:T(8,128)(2,1)S(1)}, bf16[16,256,512]{2,1,0:T(8,128)(2,1)}, u32[]{:S(2)}) copy-start(bf16[16,256,512]{2,1,0:T(8,128)(2,1)} %gather_fusion.2) | copy-start | bytes 12582916
  152.1 5.0 %copy-start.6 = (bf16[16,2,32,256]{3,2,0,1:T(8,128)(2,1)S(1)}, bf16[16,2,32,256]{3,2,0,1:T(8,128)(2,1)}, u32[]{:S(2)}) copy-start(bf16[16,2,32,256]{3,2,0,1:T(8,128)(2,1)} %get-tuple-element.101) | copy-start | bytes 1572868
  157.1 3.4 %copy-start = (bf16[16,256,512]{2,1,0:T(8,128)(2,1)S(1)}, bf16[16,256,512]{2,1,0:T(8,128)(2,1)}, u32[]{:S(2)}) copy-start(bf16[16,256,512]{2,1,0:T(8,128)(2,1)} %gather_fusion.1) | copy-start | bytes 12582916
  208.3 60.8 %reduce-scatter.5.cloned.1.call-start = ((), (), s32[]{:S(2)}) async-start(), calls=%async_computation.4 | async-start | bytes 1572864 | tf_op jit(solution)/shard_map/reduce_scatter | solution.py:77
  255.2 5.2 %copy-start.2 = (bf16[2,256,512]{2,1,0:T(8,128)(2,1)S(1)}, bf16[2,256,512]{2,1,0:T(8,128)(2,1)}, u32[]{:S(2)}) copy-start(bf16[2,256,512]{2,1,0:T(8,128)(2,1)} %param.11) | copy-start | bytes 1572868
  256.5 10.8 %copy-start.5 = (bf16[2,3,256,256]{3,2,1,0:T(8,128)(2,1)S(1)}, bf16[2,3,256,256]{3,2,1,0:T(8,128)(2,1)}, u32[]{:S(2)}) copy-start(bf16[2,3,256,256]{3,2,1,0:T(8,128)(2,1)} %get-tuple-element.77) | copy-start | bytes 2359300
Sparse Core Ops, SparseCore 0:
  10.1 125.7 all-gather.1
  208.4 6.5 reduce-scatter.2
  256.6 6.5 reduce-scatter.4
where the time goes:
time: 279 us; the launch traced here: 278 us
  waiting for transfers between devices  109 us (39%)
  other arithmetic  59.4 us (21%)
  local copies, waits for them, and re-layouts  53 us (19%)
  matrix products  30.8 us (11%)
  between operations  14 us (5%)
  starting transfers between devices  12.3 us (4%)
    all_gather x1, waiting for transfers between devices, shards(): gathered = lax.all_gather(incident, 'row', axis=1, tiled=True)  108 us
    scatter-add x2, other arithmetic, add_group(): return far_sum.at[rows_group].add(contrib)  21.5 us
    sub x5, other arithmetic, combine_parts(): real_prod[..., :half_width] - imag_prod[..., half_width:]  20 us
    concatenate x2, local copies, waits for them, and re-layouts, combine_parts(): jnp.concatenate([real_prod[..., :half_width] - imag_prod[..., half_width:...  18.5 us
    concatenate x2, other arithmetic, combine_parts(): jnp.concatenate([real_prod[..., :half_width] - imag_prod[..., half_width:...  12.5 us
    ppermute x4, starting transfers between devices, from_behind(): return lax.ppermute(value, axis, pairs)  12.1 us
    gather x2, local copies, waits for them, and re-layouts, add_group(): slot_tiles = jnp.take(wave_tiles, cols_group, axis=0)  10 us
    dot_general x2, matrix products, add_group(): jnp.einsum('fkp,fkc->fpc', u_group[:, 1], coefficients, preferred_element...  9.75 us
  transfers between devices with their start and end apart: 7, of which 1 were waited for; matrix products, arithmetic and copies ran while one was open for 51% of the time, Pallas kernels for 0%

commit v1 on v0

--- a/solution.py
+++ b/solution.py
@@ -1,7 +1,14 @@
+import functools
+
 import jax
 import jax.numpy as jnp
 from jax import lax
+from jax.experimental import pallas as pl
+from jax.experimental.pallas import tpu as pltpu
 from jax.sharding import PartitionSpec as P
+
+MESH = pl.DeviceIdType.MESH
+UP, DOWN, ALONG_Y, ALONG_X = range(4)
 
 
 def from_behind(value, axis, steps):
@@ -77,7 +84,7 @@
     return lax.psum_scatter(flat_rows, "col", scatter_dimension=0, tiled=True)
 
 
-def shards(incident, near_tiles, near_offsets, far_row, far_col, far_rank, far_count, far_u, far_v):
+def generic_shards(incident, near_tiles, near_offsets, far_row, far_col, far_rank, far_count, far_u, far_v):
     wave_count, tile_rows, columns = incident.shape
     row_blocks = lax.axis_size("col")
     slot_count = far_row.shape[2]
@@ -123,6 +130,318 @@
     return jnp.stack(outputs, axis=0).astype(jnp.bfloat16)
 
 
+def turned(block):
+    half = block.shape[-1] // 2
+    return jnp.concatenate([-block[:, half:], block[:, :half]], axis=-1)
+
+
+def fused_kernel(
+    depth, slot_ref, offset_ref, x_ref, near_hbm, u_hbm, v_hbm, out_ref,
+    tiles, near_buf, u_buf, v_buf, u_dense, coef, outgoing, incoming, total,
+    recv_sem, send_sem, pair_sem, sum_send, sum_recv, load_sem,
+):
+    waves = x_ref.shape[0]
+    row_count = depth * 4
+    rank_rows = v_buf.shape[3]
+    r = lax.axis_index("row")
+    c = lax.axis_index("col")
+    z, y, x = r // 4, (r // 2) % 2, r % 2
+    own_slot, edge_slot = row_count, row_count + 1
+    edge_tile = (r + 1 - 2 * c + row_count) % row_count
+
+    def row_of(tz, ty, tx):
+        return (tz * 2 + ty) * 2 + tx
+
+    loads = [
+        pltpu.make_async_copy(v_hbm.at[0, 0], v_buf, load_sem.at[0]),
+        pltpu.make_async_copy(u_hbm.at[0, 0], u_buf, load_sem.at[1]),
+        pltpu.make_async_copy(near_hbm.at[0], near_buf, load_sem.at[2]),
+    ]
+    for load in loads:
+        load.start()
+
+    barrier = pltpu.get_barrier_semaphore()
+    greeted = (
+        (row_of((z + 1) % depth, y, x), c),
+        (row_of((z + depth - 1) % depth, y, x), c),
+        (row_of(z, 1 - y, x), c),
+        (row_of(z, y, 1 - x), c),
+        (r, 1 - c),
+    )
+    for device in greeted:
+        pl.semaphore_signal(barrier, inc=1, device_id=device, device_id_type=MESH)
+    pl.semaphore_wait(barrier, len(greeted))
+
+    def hop(wave, tile, link, source=None, step=None):
+        if step is None:
+            step = 1 if link == UP else -1
+        target = {
+            ALONG_Y: (z, 1 - y, x),
+            ALONG_X: (z, y, 1 - x),
+        }.get(link if isinstance(link, int) else None)
+        if target is None:
+            target = (jnp.minimum(jnp.maximum(z + step, 0), depth - 1), y, x)
+        return pltpu.make_async_remote_copy(
+            src_ref=tiles.at[wave, tile] if source is None else source,
+            dst_ref=tiles.at[wave, tile],
+            send_sem=send_sem.at[wave, tile, link],
+            recv_sem=recv_sem.at[wave, tile],
+            device_id=(row_of(*target), c),
+            device_id_type=MESH,
+        )
+
+    def to_pair(wave, source, slot):
+        return pltpu.make_async_remote_copy(
+            src_ref=source,
+            dst_ref=tiles.at[wave, slot],
+            send_sem=pair_sem.at[wave, slot - row_count],
+            recv_sem=recv_sem.at[wave, slot],
+            device_id=(r, 1 - c),
+            device_id_type=MESH,
+        )
+
+    def first_link(wave):
+        return ALONG_Y if wave % 2 == 0 else ALONG_X
+
+    def second_link(wave):
+        return ALONG_X if wave % 2 == 0 else ALONG_Y
+
+    def project(wave, tile):
+        block = tiles[wave, tile]
+        row_blocks = slot_ref.shape[1]
+        factors = [
+            v_buf[wave, slot_ref[0, a, tile]].reshape(2 * rank_rows, -1) for a in range(row_blocks)
+        ]
+        prod = jnp.dot(
+            jnp.concatenate(factors, axis=0), block, preferred_element_type=jnp.float32
+        )
+        ids = lax.broadcasted_iota(jnp.int32, (rank_rows, block.shape[1]), 0)
+        for a in range(row_blocks):
+            at = 2 * rank_rows * a
+            both = combine_parts(prod[at:at + rank_rows], prod[at + rank_rows:at + 2 * rank_rows])
+            both = jnp.where(ids < slot_ref[1, a, tile], both, 0.0)
+            coef[wave, a, 0, tile] = both.astype(jnp.bfloat16)
+            coef[wave, a, 1, tile] = turned(both).astype(jnp.bfloat16)
+
+    def arrive(wave, tile):
+        pltpu.make_async_copy(tiles.at[wave, tile], tiles.at[wave, tile], recv_sem.at[wave, tile]).wait()
+
+    def share_edge(wave, tile):
+        @pl.when(tile == edge_tile)
+        def _():
+            to_pair(wave, tiles.at[wave, tile], edge_slot).start()
+
+    for wave in range(waves):
+        own = x_ref.at[wave]
+        hop(wave, r, first_link(wave), own).start()
+
+        @pl.when(z < depth - 1)
+        def _():
+            hop(wave, r, UP, own).start()
+
+        @pl.when(z > 0)
+        def _():
+            hop(wave, r, DOWN, own).start()
+
+    for wave in range(waves):
+        own = x_ref.at[wave]
+        hop(wave, r, second_link(wave), own).start()
+        to_pair(wave, own, own_slot).start()
+        tiles[wave, r] = x_ref[wave]
+    for load in loads:
+        load.wait()
+
+    def place_u(tile, carry):
+        for wave in range(waves):
+            for a in range(slot_ref.shape[1]):
+                factor = u_buf[wave, slot_ref[0, a, tile]]
+                u_dense[wave, a, 0, tile] = factor[0]
+                u_dense[wave, a, 1, tile] = factor[1]
+        return carry
+
+    lax.fori_loop(0, row_count, place_u, 0)
+    for wave in range(waves):
+        project(wave, r)
+
+    level_count = 2 * depth - 1
+    lag = 2
+
+    def level_of(step):
+        sign = 1 - 2 * (step % 2)
+        return z + sign * ((step + 1) // 2), sign
+
+    def inside(level):
+        return (level >= 0) & (level < depth)
+
+    def spread(step, carry):
+        level, sign = level_of(step)
+
+        @pl.when((step < level_count) & inside(level))
+        def _():
+            tile = row_of(level, y, x)
+            for wave in range(waves):
+                arrive(wave, tile)
+
+                @pl.when(inside(z - sign))
+                def _():
+                    hop(wave, tile, (1 + sign) // 2, step=-sign).start()
+
+                hop(wave, tile, first_link(wave)).start()
+                hop(wave, tile, second_link(wave)).start()
+                share_edge(wave, tile)
+            for wave in range(waves):
+                project(wave, tile)
+
+        behind, _ = level_of(jnp.maximum(step - lag, 0))
+
+        @pl.when((step >= lag) & inside(behind))
+        def _():
+            for wave in range(waves):
+                tile = row_of(behind, 1 - y, x) if wave % 2 == 0 else row_of(behind, y, 1 - x)
+                arrive(wave, tile)
+                hop(wave, tile, second_link(wave)).start()
+                share_edge(wave, tile)
+                project(wave, tile)
+
+        return carry
+
+    lax.fori_loop(1, level_count + lag, spread, 0)
+
+    def finish(step, carry):
+        level, _ = level_of(step % level_count)
+        far_corner = step // level_count
+
+        @pl.when(inside(level))
+        def _():
+            for wave in range(waves):
+                if wave % 2 == 0:
+                    tile = row_of(level, y + far_corner * (1 - 2 * y), 1 - x)
+                else:
+                    tile = row_of(level, 1 - y, x + far_corner * (1 - 2 * x))
+                arrive(wave, tile)
+                share_edge(wave, tile)
+                project(wave, tile)
+
+        return carry
+
+    lax.fori_loop(0, 2 * level_count, finish, 0)
+
+    def far_sum(wave, a):
+        left = u_dense[wave, a].reshape(-1, u_dense.shape[-1])
+        right = coef[wave, a].reshape(-1, coef.shape[-1])
+        return lax.dot_general(
+            left, right, (((0,), (0,)), ((), ())), preferred_element_type=jnp.float32
+        )
+
+    def send_sum(wave):
+        return pltpu.make_async_remote_copy(
+            src_ref=outgoing.at[wave],
+            dst_ref=incoming.at[wave],
+            send_sem=sum_send.at[wave],
+            recv_sem=sum_recv.at[wave],
+            device_id=(r, 1 - c),
+            device_id_type=MESH,
+        )
+
+    def fill(wave, carry):
+        outgoing[wave] = far_sum(wave, 1 - c)
+        return carry
+
+    lax.fori_loop(0, waves, fill, 0)
+    for wave in range(waves):
+        arrive(wave, own_slot)
+        arrive(wave, edge_slot)
+
+    def place_of(offset):
+        even = (r + offset // 2 + row_count) % row_count
+        same_chip = offset == 1 - 2 * c
+        return jnp.where(offset % 2 == 0, even, jnp.where(same_chip, own_slot, edge_slot))
+
+    def own_rows(wave, carry):
+        send_sum(wave).start()
+        value = far_sum(wave, c)
+        for n in range(near_buf.shape[1]):
+            block = tiles[wave, place_of(offset_ref[n])]
+            value += jnp.dot(near_buf[wave, n, 0], block, preferred_element_type=jnp.float32)
+            value += jnp.dot(
+                near_buf[wave, n, 1], turned(block), preferred_element_type=jnp.float32
+            )
+        total[wave] = value
+        return carry
+
+    lax.fori_loop(0, waves, own_rows, 0)
+    for wave in range(waves):
+        send_sum(wave).wait()
+        out_ref[wave] = (total[wave] + incoming[wave]).astype(out_ref.dtype)
+
+    for wave in range(waves):
+        to_pair(wave, x_ref.at[wave], own_slot).wait_send()
+        to_pair(wave, x_ref.at[wave], edge_slot).wait_send()
+
+    def drain(level, carry):
+        tile = row_of(level, y, x)
+        for wave in range(waves):
+            hop(wave, tile, ALONG_Y).wait_send()
+            hop(wave, tile, ALONG_X).wait_send()
+
+            @pl.when((level <= z) & (z < depth - 1))
+            def _():
+                hop(wave, tile, UP).wait_send()
+
+            @pl.when((level >= z) & (z > 0))
+            def _():
+                hop(wave, tile, DOWN).wait_send()
+
+            passed = row_of(level, 1 - y, x) if wave % 2 == 0 else row_of(level, y, 1 - x)
+            hop(wave, passed, second_link(wave)).wait_send()
+        return carry
+
+    lax.fori_loop(0, depth, drain, 0)
+
+
+def fused_shards(incident, near_tiles, near_offsets, far_row, far_col, far_rank, far_count, far_u, far_v):
+    waves, tile_rows, columns = incident.shape
+    row_count, row_blocks = lax.axis_size("row"), lax.axis_size("col")
+    slots, rank_rows = far_u.shape[3], far_u.shape[5]
+    near_slots = near_tiles.shape[2]
+    slot_ids = jnp.arange(slots, dtype=jnp.int32)
+    block_key = far_row[0, 0] * row_count + far_col[0, 0]
+    live = slot_ids < far_count[0, 0]
+    match = (block_key[:, None] == jnp.arange(row_blocks * row_count, dtype=jnp.int32)[None, :]) & live[:, None]
+    stacked = jnp.stack([slot_ids, far_rank[0, 0]], axis=0)
+    table = jnp.sum(jnp.where(match[None], stacked[:, :, None], 0), axis=1)
+    table = table.reshape(2, row_blocks, row_count)
+    bf16, f32 = jnp.bfloat16, jnp.float32
+    any_space = pl.BlockSpec(memory_space=pl.ANY)
+    smem = pl.BlockSpec(memory_space=pltpu.SMEM)
+    vmem = pl.BlockSpec(memory_space=pltpu.VMEM)
+    dma = pltpu.SemaphoreType.DMA
+    return pl.pallas_call(
+        functools.partial(fused_kernel, row_count // 4),
+        out_shape=jax.ShapeDtypeStruct(incident.shape, bf16),
+        in_specs=[smem, smem, vmem, any_space, any_space, any_space],
+        out_specs=vmem,
+        scratch_shapes=[
+            pltpu.VMEM((waves, row_count + 2, tile_rows, columns), bf16),
+            pltpu.VMEM((waves, near_slots, 2, tile_rows, tile_rows), bf16),
+            pltpu.VMEM((waves, slots, 2, rank_rows, tile_rows), bf16),
+            pltpu.VMEM((waves, slots, 2, rank_rows, tile_rows), bf16),
+            pltpu.VMEM((waves, row_blocks, 2, row_count, rank_rows, tile_rows), bf16),
+            pltpu.VMEM((waves, row_blocks, 2, row_count, rank_rows, columns), bf16),
+            pltpu.VMEM((waves, tile_rows, columns), f32),
+            pltpu.VMEM((waves, tile_rows, columns), f32),
+            pltpu.VMEM((waves, tile_rows, columns), f32),
+            dma((waves, row_count + 2)),
+            dma((waves, row_count, 4)),
+            dma((waves, 2)),
+            dma((waves,)),
+            dma((waves,)),
+            dma((3,)),
+        ],
+        compiler_params=pltpu.CompilerParams(collective_id=0, has_side_effects=True),
+    )(table, near_offsets[0], incident, near_tiles, far_u, far_v)
+
+
 def solution(mesh):
     in_specs = (
         P(None, ("row", "col"), None),
@@ -136,4 +455,6 @@
         P("row", "col", None, None, None, None, None),
     )
     out_specs = P(None, ("row", "col"), None)
+    paired = mesh.shape["col"] == 2 and mesh.shape["row"] % 4 == 0 and mesh.shape["row"] > 4
+    shards = fused_shards if paired else generic_shards
     return jax.shard_map(shards, mesh=mesh, in_specs=in_specs, out_specs=out_specs, check_vma=False)

time: 279 us -> 86.7 us (0.31)
  waiting for transfers between devices: 109 us -> 0 us
  Pallas kernels: 0 us -> 81.8 us
  other arithmetic: 59.4 us -> 1.51 us
  local copies, waits for them, and re-layouts: 53 us -> 2.53 us
  matrix products: 30.8 us -> 0 us
  between operations: 14 us -> 0.67 us
  starting transfers between devices: 12.3 us -> 0 us
    all_gather x1 -> x0, waiting for transfers between devices: 108 us -> none  [shards(): gathered = lax.all_gather(incident, 'row', axis=1, tiled=True)]
    pallas_call x0 -> x1, Pallas kernels: none -> 81.8 us  [fused_shards(): pl.pallas_call(functools.partial(fused_kernel, row_count // 4), out_shape...]
    dot_general x10 -> x0, matrix products: 30.8 us -> none  [the longest x2 9.75 us: add_group(): jnp.einsum('fkp,fkc->fpc', u_group[:, 1], coefficients, preferred_element...]
    scatter-add x2 -> x0, other arithmetic: 21.5 us -> none  [add_group(): return far_sum.at[rows_group].add(contrib)]
    sub x5 -> x0, other arithmetic: 20 us -> none  [combine_parts(): real_prod[..., :half_width] - imag_prod[..., half_width:]]
    concatenate x2 -> x0, local copies, waits for them, and re-layouts: 18.5 us -> none  [combine_parts(): jnp.concatenate([real_prod[..., :half_width] - imag_prod[..., half_width:...]
    concatenate x2 -> x0, other arithmetic: 12.5 us -> none  [combine_parts(): jnp.concatenate([real_prod[..., :half_width] - imag_prod[..., half_width:...]
    gather x3 -> x0, local copies, waits for them, and re-layouts: 12.4 us -> none  [the longest x2 10 us: add_group(): slot_tiles = jnp.take(wave_tiles, cols_group, axis=0)]
  transfers between devices with their start and end apart: 7 -> 0, of which waited for: 1 -> 0; matrix products, arithmetic and copies ran while one was open for 51% -> 0% of each run, Pallas kernels for 0% -> 0%
where the time goes in v1:
time: 86.7 us; the launch traced here: 86.5 us
  Pallas kernels  81.8 us (94%)
  local copies, waits for them, and re-layouts  2.53 us (3%)
  other arithmetic  1.51 us (2%)
    pallas_call x1, Pallas kernels, fused_shards(): pl.pallas_call(functools.partial(fused_kernel, row_count // 4), out_shape...  81.8 us
    unnamed x1, local copies, waits for them, and re-layouts  1.87 us

profile of v1, /device:TPU:0, one launch (start us, length us, event | category | flops | bytes accessed | tf_op | source)
XLA Modules:
  0.0 86.5 jit_solution(10378470831919575123)
XLA Ops:
  0.7 0.7 add_bitcast_fusion
  1.3 0.7 pad_add_fusion
  2.0 0.1 fusion
  2.1 0.1 select_reduce_fusion
  2.2 0.7 reshape.53.slot_ref
  2.8 81.8 %shard_map.91 = bf16[2,256,512]{2,1,0:T(8,128)(2,1)} custom-call(s32[2,2,16]{2,1,0:T(2,128)} %reshape.53.slot_ref, s32[3]{0:T(128)} %bitcast.6, bf16[2,256,512]{2,1,0:T(8,128)(2,1)} %x_ref.1, bf16[1,2,3,2,256,256]{5,4,3,2,1,0:T(8,128)(2,1)} %near_hbm.1, bf16[1,1,2,16,2,32,256]{6,5,4,3,2,1,0:T(8,128)(2,1)} %u_hbm.1, bf16[1,1,2,16,2,32,256]{6,5,4,3,2,1,0:T(8,128)(2,1)} %v_hbm.1), custom_call_target="tpu_custom_call" | custom-call | tf_op jit(solution)/shard_map/pallas_call | solution.py:419
  84.6 1.9 %copy.12 = bf16[2,256,512]{2,1,0:T(8,128)(2,1)} copy(bf16[2,256,512]{2,1,0:T(8,128)(2,1)} %shard_map.91) | data formatting | bytes 1048576
  (2 shorter events, 0.0 us)

commit v2 on v1

--- a/solution.py
+++ b/solution.py
@@ -137,17 +137,22 @@
 
 def fused_kernel(
     depth, slot_ref, offset_ref, x_ref, near_hbm, u_hbm, v_hbm, out_ref,
-    tiles, near_buf, u_buf, v_buf, u_dense, coef, outgoing, incoming, total,
-    recv_sem, send_sem, pair_sem, sum_send, sum_recv, load_sem,
+    tiles, near_buf, u_buf, v_buf, u_dense, coef, v_out, v_in, coef_out, outgoing, incoming, total,
+    recv_sem, send_sem, pair_sem, v_send, v_recv, c_send, c_recv, sum_send, sum_recv, load_sem,
 ):
     waves = x_ref.shape[0]
     row_count = depth * 4
+    row_blocks = slot_ref.shape[1]
     rank_rows = v_buf.shape[3]
     r = lax.axis_index("row")
     c = lax.axis_index("col")
     z, y, x = r // 4, (r // 2) % 2, r % 2
     own_slot, edge_slot = row_count, row_count + 1
     edge_tile = (r + 1 - 2 * c + row_count) % row_count
+    side = 2 * x - 1
+    partner = r + 2 * (1 - 2 * y)
+    corner = (r + side + row_count) % row_count
+    partner_corner = (partner + side + row_count) % row_count
 
     def row_of(tz, ty, tx):
         return (tz * 2 + ty) * 2 + tx
@@ -164,7 +169,7 @@
     greeted = (
         (row_of((z + 1) % depth, y, x), c),
         (row_of((z + depth - 1) % depth, y, x), c),
-        (row_of(z, 1 - y, x), c),
+        (partner, c),
         (row_of(z, y, 1 - x), c),
         (r, 1 - c),
     )
@@ -172,43 +177,63 @@
         pl.semaphore_signal(barrier, inc=1, device_id=device, device_id_type=MESH)
     pl.semaphore_wait(barrier, len(greeted))
 
-    def hop(wave, tile, link, source=None, step=None):
-        if step is None:
-            step = 1 if link == UP else -1
-        target = {
-            ALONG_Y: (z, 1 - y, x),
-            ALONG_X: (z, y, 1 - x),
-        }.get(link if isinstance(link, int) else None)
-        if target is None:
-            target = (jnp.minimum(jnp.maximum(z + step, 0), depth - 1), y, x)
-        return pltpu.make_async_remote_copy(
-            src_ref=tiles.at[wave, tile] if source is None else source,
-            dst_ref=tiles.at[wave, tile],
-            send_sem=send_sem.at[wave, tile, link],
-            recv_sem=recv_sem.at[wave, tile],
-            device_id=(row_of(*target), c),
-            device_id_type=MESH,
-        )
-
-    def to_pair(wave, source, slot):
+    def copy_to(source, target, sent, received, device):
         return pltpu.make_async_remote_copy(
             src_ref=source,
-            dst_ref=tiles.at[wave, slot],
-            send_sem=pair_sem.at[wave, slot - row_count],
-            recv_sem=recv_sem.at[wave, slot],
-            device_id=(r, 1 - c),
+            dst_ref=target,
+            send_sem=sent,
+            recv_sem=received,
+            device_id=device,
             device_id_type=MESH,
         )
 
-    def first_link(wave):
-        return ALONG_Y if wave % 2 == 0 else ALONG_X
-
-    def second_link(wave):
-        return ALONG_X if wave % 2 == 0 else ALONG_Y
+    def hop(wave, tile, link, row, source=None):
+        here = tiles.at[wave, tile]
+        return copy_to(
+            here if source is None else source,
+            here,
+            send_sem.at[wave, tile, link],
+            recv_sem.at[wave, tile],
+            (row, c),
+        )
+
+    def along_z(wave, tile, step, source=None):
+        target = jnp.minimum(jnp.maximum(z + step, 0), depth - 1)
+        return hop(wave, tile, (1 - step) // 2, row_of(target, y, x), source)
+
+    def along_x(wave, tile, source=None):
+        return hop(wave, tile, ALONG_X, row_of(z, y, 1 - x), source)
+
+    def along_y(wave, tile, source=None):
+        return hop(wave, tile, ALONG_Y, partner, source)
+
+    def to_pair(wave, source, slot):
+        return copy_to(
+            source,
+            tiles.at[wave, slot],
+            pair_sem.at[wave, slot - row_count],
+            recv_sem.at[wave, slot],
+            (r, 1 - c),
+        )
+
+    def send_v(place):
+        return copy_to(
+            v_out.at[place], v_in.at[place], v_send.at[place], v_recv.at[place], (partner, c)
+        )
+
+    def send_coef(place, tile):
+        return copy_to(
+            coef_out.at[place], coef.at[0, tile], c_send.at[place], c_recv.at[place], (partner, c)
+        )
+
+    rank_ids = lax.broadcasted_iota(jnp.int32, (rank_rows, v_buf.shape[4]), 0)
+
+    def complex_rows(prod, a):
+        at = 2 * rank_rows * a
+        return combine_parts(prod[at:at + rank_rows], prod[at + rank_rows:at + 2 * rank_rows])
 
     def project(wave, tile):
         block = tiles[wave, tile]
-        row_blocks = slot_ref.shape[1]
         factors = [
             v_buf[wave, slot_ref[0, a, tile]].reshape(2 * rank_rows, -1) for a in range(row_blocks)
         ]
@@ -217,11 +242,36 @@
         )
         ids = lax.broadcasted_iota(jnp.int32, (rank_rows, block.shape[1]), 0)
         for a in range(row_blocks):
-            at = 2 * rank_rows * a
-            both = combine_parts(prod[at:at + rank_rows], prod[at + rank_rows:at + 2 * rank_rows])
-            both = jnp.where(ids < slot_ref[1, a, tile], both, 0.0)
-            coef[wave, a, 0, tile] = both.astype(jnp.bfloat16)
-            coef[wave, a, 1, tile] = turned(both).astype(jnp.bfloat16)
+            both = jnp.where(ids < slot_ref[1, a, tile], complex_rows(prod, a), 0.0)
+            coef[0, tile, wave, a] = both.astype(jnp.bfloat16)
+            coef[1, tile, wave, a] = turned(both).astype(jnp.bfloat16)
+
+    def serve(place, tile):
+        for wave in range(waves):
+            left = v_in[place, wave].reshape(row_blocks * 2 * rank_rows, -1)
+            prod = jnp.dot(left, tiles[wave, tile], preferred_element_type=jnp.float32)
+            for a in range(row_blocks):
+                coef_out[place, wave, a] = complex_rows(prod, a).astype(jnp.bfloat16)
+
+    def use_tile(level, tx):
+        tile, place = row_of(level, y, tx), level * 2 + tx
+
+        @pl.when(tile == partner_corner)
+        def _():
+            for wave in range(waves):
+                along_y(wave, tile).start()
+
+        @pl.when(tile != partner_corner)
+        def _():
+            send_v(place).wait_recv()
+            serve(place, tile)
+
+        for wave in range(waves):
+            project(wave, tile)
+
+        @pl.when(tile != partner_corner)
+        def _():
+            send_coef(place, tile).start()
 
     def arrive(wave, tile):
         pltpu.make_async_copy(tiles.at[wave, tile], tiles.at[wave, tile], recv_sem.at[wave, tile]).wait()
@@ -231,47 +281,70 @@
         def _():
             to_pair(wave, tiles.at[wave, tile], edge_slot).start()
 
+    level_count = 2 * depth - 1
+    lag = 2
+
+    def level_of(step):
+        sign = 1 - 2 * (step % 2)
+        return z + sign * ((step + 1) // 2), sign
+
+    def inside(level):
+        return (level >= 0) & (level < depth)
+
     for wave in range(waves):
         own = x_ref.at[wave]
-        hop(wave, r, first_link(wave), own).start()
+        along_x(wave, r, own).start()
 
         @pl.when(z < depth - 1)
         def _():
-            hop(wave, r, UP, own).start()
+            along_z(wave, r, 1, own).start()
 
         @pl.when(z > 0)
         def _():
-            hop(wave, r, DOWN, own).start()
-
-    for wave in range(waves):
-        own = x_ref.at[wave]
-        hop(wave, r, second_link(wave), own).start()
+            along_z(wave, r, -1, own).start()
+
         to_pair(wave, own, own_slot).start()
         tiles[wave, r] = x_ref[wave]
-    for load in loads:
+
+    loads[0].wait()
+
+    def place_v(place, carry):
+        tile = row_of(place // 2, 1 - y, place % 2)
+        for wave in range(waves):
+            for a in range(row_blocks):
+                factor = v_buf[wave, slot_ref[0, a, tile]]
+                for part in range(2):
+                    kept = factor[part].astype(jnp.float32)
+                    kept = jnp.where(rank_ids < slot_ref[1, a, tile], kept, 0.0)
+                    v_out[place, wave, a, part] = kept.astype(jnp.bfloat16)
+        return carry
+
+    lax.fori_loop(0, 2 * depth, place_v, 0)
+
+    def push_v(step, carry):
+        level, _ = level_of(step // 2)
+        tx = (x + step) % 2
+
+        @pl.when(inside(level) & (row_of(level, 1 - y, tx) != corner))
+        def _():
+            send_v(level * 2 + tx).start()
+
+        return carry
+
+    lax.fori_loop(0, 2 * level_count, push_v, 0)
+
+    for load in loads[1:]:
         load.wait()
 
     def place_u(tile, carry):
         for wave in range(waves):
-            for a in range(slot_ref.shape[1]):
+            for a in range(row_blocks):
                 factor = u_buf[wave, slot_ref[0, a, tile]]
                 u_dense[wave, a, 0, tile] = factor[0]
                 u_dense[wave, a, 1, tile] = factor[1]
         return carry
 
     lax.fori_loop(0, row_count, place_u, 0)
-    for wave in range(waves):
-        project(wave, r)
-
-    level_count = 2 * depth - 1
-    lag = 2
-
-    def level_of(step):
-        sign = 1 - 2 * (step % 2)
-        return z + sign * ((step + 1) // 2), sign
-
-    def inside(level):
-        return (level >= 0) & (level < depth)
 
     def spread(step, carry):
         level, sign = level_of(step)
@@ -279,68 +352,63 @@
         @pl.when((step < level_count) & inside(level))
         def _():
             tile = row_of(level, y, x)
+
+            @pl.when(step > 0)
+            def _():
+                for wave in range(waves):
+                    arrive(wave, tile)
+
+                    @pl.when(inside(z - sign))
+                    def _():
+                        along_z(wave, tile, -sign).start()
+
+                    along_x(wave, tile).start()
+
+            use_tile(level, x)
+
+        behind, _ = level_of(jnp.maximum(step - lag, 0))
+
+        @pl.when((step >= lag) & inside(behind))
+        def _():
+            tile = row_of(behind, y, 1 - x)
             for wave in range(waves):
                 arrive(wave, tile)
-
-                @pl.when(inside(z - sign))
-                def _():
-                    hop(wave, tile, (1 + sign) // 2, step=-sign).start()
-
-                hop(wave, tile, first_link(wave)).start()
-                hop(wave, tile, second_link(wave)).start()
                 share_edge(wave, tile)
+            use_tile(behind, 1 - x)
+
+        return carry
+
+    lax.fori_loop(0, level_count + lag, spread, 0)
+
+    for wave in range(waves):
+        arrive(wave, corner)
+        share_edge(wave, corner)
+        project(wave, corner)
+
+    def finish(place, carry):
+        tile = row_of(place // 2, 1 - y, place % 2)
+
+        @pl.when(tile != corner)
+        def _():
+            send_coef(place, tile).wait_recv()
             for wave in range(waves):
-                project(wave, tile)
-
-        behind, _ = level_of(jnp.maximum(step - lag, 0))
-
-        @pl.when((step >= lag) & inside(behind))
-        def _():
-            for wave in range(waves):
-                tile = row_of(behind, 1 - y, x) if wave % 2 == 0 else row_of(behind, y, 1 - x)
-                arrive(wave, tile)
-                hop(wave, tile, second_link(wave)).start()
-                share_edge(wave, tile)
-                project(wave, tile)
-
-        return carry
-
-    lax.fori_loop(1, level_count + lag, spread, 0)
-
-    def finish(step, carry):
-        level, _ = level_of(step % level_count)
-        far_corner = step // level_count
-
-        @pl.when(inside(level))
-        def _():
-            for wave in range(waves):
-                if wave % 2 == 0:
-                    tile = row_of(level, y + far_corner * (1 - 2 * y), 1 - x)
-                else:
-                    tile = row_of(level, 1 - y, x + far_corner * (1 - 2 * x))
-                arrive(wave, tile)
-                share_edge(wave, tile)
-                project(wave, tile)
-
-        return carry
-
-    lax.fori_loop(0, 2 * level_count, finish, 0)
+                for a in range(row_blocks):
+                    coef[1, tile, wave, a] = turned(coef[0, tile, wave, a])
+
+        return carry
+
+    lax.fori_loop(0, 2 * depth, finish, 0)
 
     def far_sum(wave, a):
         left = u_dense[wave, a].reshape(-1, u_dense.shape[-1])
-        right = coef[wave, a].reshape(-1, coef.shape[-1])
+        right = coef[:, :, wave, a].reshape(-1, coef.shape[-1])
         return lax.dot_general(
             left, right, (((0,), (0,)), ((), ())), preferred_element_type=jnp.float32
         )
 
     def send_sum(wave):
-        return pltpu.make_async_remote_copy(
-            src_ref=outgoing.at[wave],
-            dst_ref=incoming.at[wave],
-            send_sem=sum_send.at[wave],
-            recv_sem=sum_recv.at[wave],
-            device_id=(r, 1 - c),
-            device_id_type=MESH,
+        return copy_to(
+            outgoing.at[wave], incoming.at[wave], sum_send.at[wave], sum_recv.at[wave], (r, 1 - c)
         )
 
     def fill(wave, carry):
@@ -377,23 +445,31 @@
     for wave in range(waves):
         to_pair(wave, x_ref.at[wave], own_slot).wait_send()
         to_pair(wave, x_ref.at[wave], edge_slot).wait_send()
+        along_y(wave, partner_corner).wait_send()
 
     def drain(level, carry):
         tile = row_of(level, y, x)
         for wave in range(waves):
-            hop(wave, tile, ALONG_Y).wait_send()
-            hop(wave, tile, ALONG_X).wait_send()
+            along_x(wave, tile).wait_send()
 
             @pl.when((level <= z) & (z < depth - 1))
             def _():
-                hop(wave, tile, UP).wait_send()
+                along_z(wave, tile, 1).wait_send()
 
             @pl.when((level >= z) & (z > 0))
             def _():
-                hop(wave, tile, DOWN).wait_send()
-
-            passed = row_of(level, 1 - y, x) if wave % 2 == 0 else row_of(level, y, 1 - x)
-            hop(wave, passed, second_link(wave)).wait_send()
+                along_z(wave, tile, -1).wait_send()
+
+        for tx in range(2):
+            place = level * 2 + tx
+
+            @pl.when(row_of(level, 1 - y, tx) != corner)
+            def _():
+                send_v(place).wait_send()
+
+            @pl.when(row_of(level, y, tx) != partner_corner)
+            def _():
+                send_coef(place, row_of(level, y, tx)).wait_send()
         return carry
 
     lax.fori_loop(0, depth, drain, 0)
@@ -427,13 +503,20 @@
             pltpu.VMEM((waves, slots, 2, rank_rows, tile_rows), bf16),
             pltpu.VMEM((waves, slots, 2, rank_rows, tile_rows), bf16),
             pltpu.VMEM((waves, row_blocks, 2, row_count, rank_rows, tile_rows), bf16),
-            pltpu.VMEM((waves, row_blocks, 2, row_count, rank_rows, columns), bf16),
+            pltpu.VMEM((2, row_count, waves, row_blocks, rank_rows, columns), bf16),
+            pltpu.VMEM((row_count // 2, waves, row_blocks, 2, rank_rows, tile_rows), bf16),
+            pltpu.VMEM((row_count // 2, waves, row_blocks, 2, rank_rows, tile_rows), bf16),
+            pltpu.VMEM((row_count // 2, waves, row_blocks, rank_rows, columns), bf16),
             pltpu.VMEM((waves, tile_rows, columns), f32),
             pltpu.VMEM((waves, tile_rows, columns), f32),
             pltpu.VMEM((waves, tile_rows, columns), f32),
             dma((waves, row_count + 2)),
             dma((waves, row_count, 4)),
             dma((waves, 2)),
+            dma((row_count // 2,)),
+            dma((row_count // 2,)),
+            dma((row_count // 2,)),
+            dma((row_count // 2,)),
             dma((waves,)),
             dma((waves,)),
             dma((3,)),

time: 86.7 us -> 77.1 us (0.89)
  Pallas kernels: 81.8 us -> 72.2 us
    pallas_call x1, Pallas kernels: 81.8 us -> 72.2 us  [fused_shards(): pl.pallas_call(functools.partial(fused_kernel, row_count // 4), out_shape...]
where the time goes in v2:
time: 77.1 us; the launch traced here: 76.9 us
  Pallas kernels  72.2 us (94%)
  local copies, waits for them, and re-layouts  2.53 us (3%)
  other arithmetic  1.51 us (2%)
    pallas_call x1, Pallas kernels, fused_shards(): pl.pallas_call(functools.partial(fused_kernel, row_count // 4), out_shape...  72.2 us
    unnamed x1, local copies, waits for them, and re-layouts  1.87 us

profile of v2, /device:TPU:0, one launch (start us, length us, event | category | flops | bytes accessed | tf_op | source)
XLA Modules:
  0.0 76.9 jit_solution(15914849861294647221)
XLA Ops:
  0.7 0.7 add_bitcast_fusion
  1.3 0.7 pad_add_fusion
  2.0 0.1 fusion
  2.1 0.1 select_reduce_fusion
  2.2 0.7 reshape.53.slot_ref
  2.8 72.2 %shard_map.91 = bf16[2,256,512]{2,1,0:T(8,128)(2,1)} custom-call(s32[2,2,16]{2,1,0:T(2,128)} %reshape.53.slot_ref, s32[3]{0:T(128)} %bitcast.6, bf16[2,256,512]{2,1,0:T(8,128)(2,1)} %x_ref.1, bf16[1,2,3,2,256,256]{5,4,3,2,1,0:T(8,128)(2,1)} %near_hbm.1, bf16[1,1,2,16,2,32,256]{6,5,4,3,2,1,0:T(8,128)(2,1)} %u_hbm.1, bf16[1,1,2,16,2,32,256]{6,5,4,3,2,1,0:T(8,128)(2,1)} %v_hbm.1), custom_call_target="tpu_custom_call" | custom-call | tf_op jit(solution)/shard_map/pallas_call | solution.py:495
  75.0 1.9 %copy.12 = bf16[2,256,512]{2,1,0:T(8,128)(2,1)} copy(bf16[2,256,512]{2,1,0:T(8,128)(2,1)} %shard_map.91) | data formatting | bytes 1048576
  (2 shorter events, 0.0 us)

commit v3 on v2

--- a/solution.py
+++ b/solution.py
@@ -198,7 +198,7 @@
         )
 
     def along_z(wave, tile, step, source=None):
-        target = jnp.minimum(jnp.maximum(z + step, 0), depth - 1)
+        target = (z + step + depth) % depth
         return hop(wave, tile, (1 - step) // 2, row_of(target, y, x), source)
 
     def along_x(wave, tile, source=None):
@@ -281,28 +281,21 @@
         def _():
             to_pair(wave, tiles.at[wave, tile], edge_slot).start()
 
-    level_count = 2 * depth - 1
     lag = 2
 
     def level_of(step):
         sign = 1 - 2 * (step % 2)
-        return z + sign * ((step + 1) // 2), sign
-
-    def inside(level):
-        return (level >= 0) & (level < depth)
+        return (z + sign * ((step + 1) // 2) + depth) % depth, sign
+
+    def reach(wave, step):
+        return depth // 2 if (step == 1) == (wave % 2 == 0) else (depth - 1) // 2
 
     for wave in range(waves):
         own = x_ref.at[wave]
         along_x(wave, r, own).start()
-
-        @pl.when(z < depth - 1)
-        def _():
-            along_z(wave, r, 1, own).start()
-
-        @pl.when(z > 0)
-        def _():
-            along_z(wave, r, -1, own).start()
-
+        for step in (1, -1):
+            if reach(wave, step) > 0:
+                along_z(wave, r, step, own).start()
         to_pair(wave, own, own_slot).start()
         tiles[wave, r] = x_ref[wave]
 
@@ -325,13 +318,13 @@
         level, _ = level_of(step // 2)
         tx = (x + step) % 2
 
-        @pl.when(inside(level) & (row_of(level, 1 - y, tx) != corner))
+        @pl.when(row_of(level, 1 - y, tx) != corner)
         def _():
             send_v(level * 2 + tx).start()
 
         return carry
 
-    lax.fori_loop(0, 2 * level_count, push_v, 0)
+    lax.fori_loop(0, 2 * depth, push_v, 0)
 
     for load in loads[1:]:
         load.wait()
@@ -349,7 +342,7 @@
     def spread(step, carry):
         level, sign = level_of(step)
 
-        @pl.when((step < level_count) & inside(level))
+        @pl.when(step < depth)
         def _():
             tile = row_of(level, y, x)
 
@@ -358,9 +351,10 @@
                 for wave in range(waves):
                     arrive(wave, tile)
 
-                    @pl.when(inside(z - sign))
-                    def _():
-                        along_z(wave, tile, -sign).start()
+                    for move in (1, -1):
+                        @pl.when((sign == -move) & ((step + 1) // 2 < reach(wave, move)))
+                        def _():
+                            along_z(wave, tile, move).start()
 
                     along_x(wave, tile).start()
 
@@ -368,7 +362,7 @@
 
         behind, _ = level_of(jnp.maximum(step - lag, 0))
 
-        @pl.when((step >= lag) & inside(behind))
+        @pl.when(step >= lag)
         def _():
             tile = row_of(behind, y, 1 - x)
             for wave in range(waves):
@@ -378,7 +372,7 @@
 
         return carry
 
-    lax.fori_loop(0, level_count + lag, spread, 0)
+    lax.fori_loop(0, depth + lag, spread, 0)
 
     for wave in range(waves):
         arrive(wave, corner)
@@ -451,14 +445,10 @@
         tile = row_of(level, y, x)
         for wave in range(waves):
             along_x(wave, tile).wait_send()
-
-            @pl.when((level <= z) & (z < depth - 1))
-            def _():
-                along_z(wave, tile, 1).wait_send()
-
-            @pl.when((level >= z) & (z > 0))
-            def _():
-                along_z(wave, tile, -1).wait_send()
+            for move in (1, -1):
+                @pl.when((move * (z - level) + depth) % depth < reach(wave, move))
+                def _():
+                    along_z(wave, tile, move).wait_send()
 
         for tx in range(2):
             place = level * 2 + tx

time: 77.1 us -> 74 us (0.960)
  Pallas kernels: 72.2 us -> 69.1 us
    pallas_call x1, Pallas kernels: 72.2 us -> 69.1 us  [fused_shards(): pl.pallas_call(functools.partial(fused_kernel, row_count // 4), out_shape...]
where the time goes in v3:
time: 74 us; the launch traced here: 73.8 us
  Pallas kernels  69.1 us (93%)
  local copies, waits for them, and re-layouts  2.53 us (3%)
  other arithmetic  1.51 us (2%)
    pallas_call x1, Pallas kernels, fused_shards(): pl.pallas_call(functools.partial(fused_kernel, row_count // 4), out_shape...  69.1 us
    unnamed x1, local copies, waits for them, and re-layouts  1.87 us

profile of v3, /device:TPU:0, one launch (start us, length us, event | category | flops | bytes accessed | tf_op | source)
XLA Modules:
  0.0 73.8 jit_solution(13702490109383889211)
XLA Ops:
  0.7 0.7 add_bitcast_fusion
  1.3 0.7 pad_add_fusion
  2.0 0.1 fusion
  2.1 0.1 select_reduce_fusion
  2.2 0.7 reshape.53.slot_ref
  2.8 69.1 %shard_map.91 = bf16[2,256,512]{2,1,0:T(8,128)(2,1)} custom-call(s32[2,2,16]{2,1,0:T(2,128)} %reshape.53.slot_ref, s32[3]{0:T(128)} %bitcast.6, bf16[2,256,512]{2,1,0:T(8,128)(2,1)} %x_ref.1, bf16[1,2,3,2,256,256]{5,4,3,2,1,0:T(8,128)(2,1)} %near_hbm.1, bf16[1,1,2,16,2,32,256]{6,5,4,3,2,1,0:T(8,128)(2,1)} %u_hbm.1, bf16[1,1,2,16,2,32,256]{6,5,4,3,2,1,0:T(8,128)(2,1)} %v_hbm.1), custom_call_target="tpu_custom_call" | custom-call | tf_op jit(solution)/shard_map/pallas_call | solution.py:485
  71.9 1.9 %copy.12 = bf16[2,256,512]{2,1,0:T(8,128)(2,1)} copy(bf16[2,256,512]{2,1,0:T(8,128)(2,1)} %shard_map.91) | data formatting | bytes 1048576
  (2 shorter events, 0.0 us)
